TPU v7x, 32 devices: a 4x4x1 block of a 4x4x8 slice. The times are simulated.
32 devices in a mesh: dp: 1 (over z), ep: 32 (over y, x, core).
Axes of the slice: x: 4, y: 4, z: 1, core: 2. Of those that a mesh axis runs over, the one named last changes fastest.
The devices are a block of a 4x4x8 slice.
Arguments:
- dispatched: bfloat16 [32, 128, 16, 2048], P('dp', 'ep')
- w_gate: bfloat16 [128, 2048, 768], P('ep')
- w_up: bfloat16 [128, 2048, 768], P('ep')
- w_down: bfloat16 [128, 768, 2048], P('ep')
- fill_count: int32 [32, 128], P('dp', 'ep')
- slot_index: int32 [4096, 8], P(('dp', 'ep'))
- expert_id: int32 [4096, 8], P(('dp', 'ep'))
- gate_weight: float32 [4096, 8], P(('dp', 'ep'))
Outputs:
- output: bfloat16 [4096, 2048], P(('dp', 'ep'))
All inputs are finite; a program needn't handle non-finite values.
Results may differ from a plain program's by a relative error of at most 0.00111.
Values are sent between devices in bfloat16 or wider.
A program may use at most 768 MiB of HBM per device.

v0:
```python
import jax
import jax.numpy as jnp
from jax import lax
from jax.sharding import PartitionSpec as P


def expert_rows(dispatched, w_gate, w_up, w_down, fill_count):
    capacity = dispatched.shape[2]
    pre_gate = jnp.einsum("secd,edf->escf", dispatched, w_gate, preferred_element_type=jnp.float32)
    pre_up = jnp.einsum("secd,edf->escf", dispatched, w_up, preferred_element_type=jnp.float32)
    hidden = (jax.nn.silu(pre_gate) * pre_up).astype(jnp.bfloat16)
    result = jnp.einsum("escf,efd->escd", hidden, w_down, preferred_element_type=jnp.float32).astype(jnp.bfloat16)
    live_mask = jnp.arange(capacity)[None, None, :] < fill_count.T[:, :, None]
    return jnp.where(live_mask[..., None], result, 0)


def solution(mesh):
    def local_step(dispatched, w_gate, w_up, w_down, fill_count, slot_index, expert_id, gate_weight):
        result = expert_rows(dispatched, w_gate, w_up, w_down, fill_count)
        returned = lax.all_to_all(result, "ep", 1, 0, tiled=True)
        flat_rows = returned.reshape(-1, returned.shape[-1])
        row_index = expert_id * dispatched.shape[2] + jnp.maximum(slot_index, 0)
        picked = jnp.take(flat_rows, row_index, axis=0)
        weight = jnp.where(slot_index >= 0, gate_weight, 0.0)
        combined = jnp.sum(weight[:, :, None] * picked.astype(jnp.float32), axis=1)
        return combined.astype(jnp.bfloat16)
    token_spec = P(("dp", "ep"))
    in_specs = (P("dp", "ep"), P("ep"), P("ep"), P("ep"), P("dp", "ep"), token_spec, token_spec, token_spec)
    return jax.shard_map(local_step, mesh=mesh, in_specs=in_specs, out_specs=token_spec, check_vma=False)
```

profile of v0, /device:TPU:103, one launch (start us, length us, event | category | flops | bytes accessed | tf_op | source)
XLA Modules:
  0.0 186.1 jit_solution(11052644352966299026)
XLA Ops:
  0.0 0.8 iota_compare_fusion
  0.8 14.3 %fusion.2 = f32[4,32,16,768]{3,2,1,0:T(8,128)} fusion(bf16[4,2048,768]{2,1,0:T(8,128)(2,1)} %param.10, bf16[32,4,16,2048]{3,2,1,0:T(8,128)(2,1)} %param.8), kind=kOutput, calls=%fused_computation.3 | convolution fusion | flops 6442450944 | bytes 27262976 | tf_op jit(solution)/shard_map/secd,edf->escf/dot_general | solution.py:10
  15.1 22.0 %convert_select_fusion = bf16[4,32,16,2048]{3,2,1,0:T(8,128)(2,1)} fusion(pred[4,32,16]{2,1,0:T(8,128)(4,1)S(1)} %iota_compare_fusion, bf16[4,768,2048]{2,1,0:T(8,128)(2,1)} %param.11, f32[4,32,16,768]{3,2,1,0:T(8,128)} %fusion.2, bf16[4,2048,768]{2,1,0:T(8,128)(2,1)} %param.9, bf16[32,4,16,2048]{3,2,1,0:T(8,128)(2,1)} %param.8), kind=kOutput, calls=%fused_computation.8 | convolution fusion | flops 12902727680 | bytes 48236544 | tf_op jit(solution)/shard_map/escf,efd->escd/dot_general | solution.py:12
  37.1 8.3 %copy.21 = bf16[4,32,16,2048]{3,2,0,1:T(8,128)(2,1)} copy(bf16[4,32,16,2048]{3,2,1,0:T(8,128)(2,1)} %convert_select_fusion) | data formatting | bytes 16777216 | tf_op jit(solution)/shard_map/jit(_where)/select_n | solution.py:14
  45.4 0.0 copy-start
  45.4 0.0 copy-start.2
  45.4 0.0 copy-start.1
  45.4 8.0 %all-to-all-start = ((bf16[4,32,16,2048]{3,2,0,1:T(8,128)(2,1)}), bf16[4,32,16,2048]{3,2,0,1:T(8,128)(2,1)}, u32[]{:S(2)}, u32[]{:S(2)}) async-start(bf16[4,32,16,2048]{3,2,0,1:T(8,128)(2,1)} %copy.21), calls=%async_computation | async-start | bytes 16777216 | tf_op jit(solution)/shard_map/all_to_all | solution.py:20
  53.4 0.0 copy-done
  53.4 0.0 copy-done.2
  53.4 0.1 copy.22
  53.5 0.1 reshape.18
  53.6 0.0 copy-done.1
  53.6 0.1 copy.17
  53.7 0.1 copy.18
  53.9 112.7 %all-to-all-done = bf16[4,32,16,2048]{3,2,0,1:T(8,128)(2,1)} async-done(((bf16[4,32,16,2048]{3,2,0,1:T(8,128)(2,1)}), bf16[4,32,16,2048]{3,2,0,1:T(8,128)(2,1)}, u32[]{:S(2)}, u32[]{:S(2)}) %all-to-all-start) | async-done | bytes 8388640 | tf_op jit(solution)/shard_map/all_to_all | solution.py:20
  166.5 13.3 %gather_fusion = bf16[1024,2048]{1,0:T(8,128)(2,1)} fusion(bf16[2048,2048]{1,0:T(8,128)(2,1)} %bitcast.9, s32[1024]{0:T(1024)S(1)} %broadcast_clamp_fusion), kind=kCustom, calls=%fused_computation | custom fusion | bytes 8392704 | tf_op jit(solution)/shard_map/jit(_take)/gather | solution.py:23
  179.8 6.3 %multiply_reduce_fusion = bf16[128,2048]{1,0:T(8,128)(2,1)} fusion(bf16[1024,2048]{1,0:T(8,128)(2,1)} %gather_fusion, f32[128,8]{1,0:T(8,128)S(1)} %copy.17, pred[128,8]{1,0:T(8,128)(4,1)S(1)} %copy.18), kind=kLoop, calls=%fused_computation.7 | loop fusion | flops 8126464 | bytes 4723712 | tf_op jit(solution)/shard_map/reduce_sum | solution.py:25
  (3 shorter events, 0.0 us)
Async XLA Ops:
  45.4 8.0 %copy-start = (s32[128,8]{0,1:T(8,128)S(1)}, s32[128,8]{0,1:T(8,128)}, u32[]{:S(2)}) copy-start(s32[128,8]{0,1:T(8,128)} %param.13) | copy-start | bytes 12292
  45.4 8.0 %copy-start.2 = (s32[128,8]{0,1:T(8,128)S(1)}, s32[128,8]{0,1:T(8,128)}, u32[]{:S(2)}) copy-start(s32[128,8]{0,1:T(8,128)} %param.14) | copy-start | bytes 12292
  45.4 8.2 %copy-start.1 = (f32[128,8]{0,1:T(8,128)S(1)}, f32[128,8]{0,1:T(8,128)}, u32[]{:S(2)}) copy-start(f32[128,8]{0,1:T(8,128)} %param.15) | copy-start | bytes 12292
  45.4 121.1 %all-to-all-start = ((bf16[4,32,16,2048]{3,2,0,1:T(8,128)(2,1)}), bf16[4,32,16,2048]{3,2,0,1:T(8,128)(2,1)}, u32[]{:S(2)}, u32[]{:S(2)}) async-start(bf16[4,32,16,2048]{3,2,0,1:T(8,128)(2,1)} %copy.21), calls=%async_computation | async-start | bytes 16777216 | tf_op jit(solution)/shard_map/all_to_all | solution.py:20
where the time goes:
time: 186 us
  waiting for transfers between devices  113 us (61%)
  matrix products  36.3 us (20%)
  local copies, waits for them, and re-layouts  22 us (12%)
  starting transfers between devices  7.99 us (4%)
  other arithmetic  7.05 us (4%)
    all_to_all x1, waiting for transfers between devices, local_step(): returned = lax.all_to_all(result, 'ep', 1, 0, tiled=True)  113 us
    dot_general x1, matrix products, expert_rows(): jnp.einsum('escf,efd->escd', hidden, w_down, preferred_element_type=jnp.f...  22 us
    dot_general x1, matrix products, expert_rows(): jnp.einsum('secd,edf->escf', dispatched, w_up, preferred_element_type=jnp...  14.3 us
    gather x1, local copies, waits for them, and re-layouts, local_step(): picked = jnp.take(flat_rows, row_index, axis=0)  13.3 us
    select_n x1, local copies, waits for them, and re-layouts, expert_rows(): return jnp.where(live_mask[..., None], result, 0)  8.27 us
    all_to_all x1, starting transfers between devices, local_step(): returned = lax.all_to_all(result, 'ep', 1, 0, tiled=True)  7.99 us
    reduce_sum x1, other arithmetic, local_step(): combined = jnp.sum(weight[:, :, None] * picked.astype(jnp.float32), axis=1)  6.27 us
  transfers between devices with their start and end apart: 1, of which 1 were waited for; matrix products, arithmetic and copies ran while one was open for 0% of the time, Pallas kernels for 0%

commit v1 on v0

v1 whole, which is shorter than its diff:
```python
import functools
import math

import jax
import jax.numpy as jnp
from jax import lax
from jax.experimental import pallas as pl
from jax.experimental.pallas import tpu as pltpu
from jax.sharding import PartitionSpec as P

MESH = pl.DeviceIdType.MESH
BF16, F32, I32 = jnp.bfloat16, jnp.float32, jnp.int32
HEAD = 4
HEADED = 3
COLS = 256
ROOM = 48
MORE = (8, 16, 24, 40)
GRANT = 64 * 1024 * 1024 - 65536
ORDER = ((2, 2), (2, 1), (2, 3), (1, 2), (3, 2), (2, 0), (0, 2), (1, 1), (3, 3), (1, 3), (3, 1), (1, 0), (3, 0), (0, 1), (0, 3))
STEP_X = sum(x << (2 * i) for i, (x, y) in enumerate(ORDER))
STEP_Y = sum(y << (2 * i) for i, (x, y) in enumerate(ORDER))


def step_to(chip, side, i):
    dx = lax.shift_right_logical(jnp.int32(STEP_X), 2 * i) & 3
    dy = lax.shift_right_logical(jnp.int32(STEP_Y), 2 * i) & 3
    return ((chip + dy * side) & (side * side - side)) + ((chip + dx) & (side - 1))


def iota(shape, dim):
    return lax.broadcasted_iota(I32, shape, dim)


def one(cond):
    return jnp.where(cond, 1.0, 0.0)


def needs(expert_t, slot_t, total, experts):
    tokens = expert_t.shape[1]
    hit = jnp.zeros((total, tokens), F32)
    for c in range(expert_t.shape[0]):
        hit = hit + one((iota((total, tokens), 0) == expert_t[c:c + 1]) & (slot_t[c:c + 1] >= 0))
    count = jnp.sum(hit, axis=1, keepdims=True)
    headed = lax.rem(iota((total, 1), 0), experts) < HEADED
    beyond = jnp.maximum(count - jnp.where(headed, float(HEAD), 0.0), 0.0)
    g, p = iota((total, total), 0), iota((total, total), 1)
    lower = one((g // (2 * experts) == p // (2 * experts)) & (p < g)).astype(BF16)
    before = jnp.dot(lower, jnp.broadcast_to(beyond, (total, 128)).astype(BF16), preferred_element_type=F32)
    return beyond, before


def place_rows(table, me, core, n, experts, cap, place):
    lanes = 2 * experts * cap
    fills = jnp.concatenate([table[me, 0:experts], table[me + 1 - 2 * core, 0:experts], jnp.zeros((128 - 2 * experts, 128), F32)])
    fills = fills.T
    k, lane = iota((128, lanes), 0), iota((128, lanes), 1)
    early = lax.rem(iota((128, 128), 1), experts) < HEADED
    extra = jnp.maximum(fills - jnp.where(early, float(HEAD), 0.0), 0.0)
    rank_k = lax.rem(k + experts * core, 2 * experts)
    rank_l = lax.rem(lane // cap + experts * core, 2 * experts)
    spread = one(k == lane // cap).astype(BF16)
    earlier = one((rank_k < rank_l) & (k < 2 * experts)).astype(BF16)
    filled = jnp.dot(fills.astype(BF16), spread, preferred_element_type=F32)
    start = jnp.dot(extra.astype(BF16), earlier, preferred_element_type=F32)
    slot = lax.rem(lane, cap)
    skip = jnp.where(lax.rem(lane // cap, experts) < HEADED, HEAD, 0)
    spot = jnp.where((slot >= skip) & (slot.astype(F32) < filled), start.astype(I32) + slot - skip, -1)
    place[...] = spot[0:n]


def token_spots(expert, slot, before, chip, side, experts):
    total, tokens = before.shape[0], expert.shape[1]
    lead = []
    for c in range(expert.shape[0]):
        hit = iota((total, tokens), 0) == expert[c:c + 1]
        lead.append(jnp.sum(jnp.where(hit, before, 0.0), axis=0, keepdims=True))
    lead = jnp.concatenate(lead, axis=0).astype(I32)
    local = lax.rem(expert, experts)
    early = local < HEADED
    in_head = early & (slot >= 0) & (slot < HEAD)
    head_spot = jnp.where(in_head, ((expert // experts) * HEADED + local) * 8 + slot, -64)
    home = expert // (2 * experts)
    order = jnp.full(expert.shape, side * side - 1, I32)
    for i, (dx, dy) in enumerate(ORDER):
        came = lax.rem(chip // side + side - dy, side) * side + lax.rem(lax.rem(chip, side) + side - dx, side)
        order = jnp.where(home == came, i, order)
    skip = jnp.where(early, HEAD, 0)
    return head_spot, order, jnp.where(slot >= skip, lead + slot - skip, -1)


def set_keys(keys, spots, weight):
    tokens = weight.shape[1]
    rows = [k.astype(F32) for k in spots] + [weight]
    rows.append(jnp.zeros((128 - len(rows) * weight.shape[0], tokens), F32))
    keys[...] = jnp.concatenate(rows).T


def mix(keys, top, first, weight, add, mix_ref, base):
    tokens = keys.shape[0]

    def tile(i, carry):
        lane = (iota((tokens, 128), 1) + (i * 128 - add)).astype(F32)
        w = jnp.zeros((tokens, 128), F32)
        for c in range(top):
            w = w + jnp.where(lane == keys[:, first + c:first + c + 1], keys[:, weight + c:weight + c + 1], 0.0)
        cols = pl.ds(pl.multiple_of(i * 128, 128), 128)
        for p, part in enumerate(split3(w)):
            mix_ref[pl.ds(base + p * tokens, tokens), cols] = part
        return carry
    lax.fori_loop(0, mix_ref.shape[1] // 128, tile, 0)


def fold(v, base, tokens):
    return v[base:base + tokens] + (v[base + tokens:base + 2 * tokens] + v[base + 2 * tokens:base + 3 * tokens])


def weigh(got, mix_ref, cols):
    rows = got.shape[0] * got.shape[1]
    v = jnp.dot(mix_ref[...], got[:, :, cols].reshape(rows, COLS), preferred_element_type=F32)
    return fold(v, 0, mix_ref.shape[0] // 3)


def main_kernel(n, fill, fill_v, expert_t, slot_t, weight_t, x, w_gate, w_up, w_down, own, other, table, branch, total,
                x_buf, gate_buf, up_buf, down_buf, hidden, mask, rows, theirs, head, head_in, note, place, keys,
                head_mix, mix_a, mix_b, pack_a, pack_b, got_a, got_b,
                load_sem, x_sem, own_sem, theirs_sem, pair_send, pair_recv, head_send, head_recv, note_send, note_recv, send_sem, recv_sem):
    me = lax.axis_index("ep")
    core = me & 1
    chip = lax.shift_right_logical(me, 1)
    chips = n // 2
    side = math.isqrt(chips)
    _, _, experts, cap, width = x.shape
    sources = n
    ffn = w_gate.shape[2]
    half = width // 2
    top, tokens = expert_t.shape
    cut = got_a.shape[1]
    rest = got_b.shape[1]
    barrier = pltpu.get_barrier_semaphore()

    def load_x(e, slot, h):
        return pltpu.make_async_copy(x.at[:, (core + 1 + h) & 1, e], x_buf.at[slot, h], x_sem.at[slot, h])

    def load_w(e, slot):
        return (
            pltpu.make_async_copy(w_gate.at[e], gate_buf.at[slot], load_sem.at[0, slot]),
            pltpu.make_async_copy(w_up.at[e], up_buf.at[slot], load_sem.at[1, slot]),
            pltpu.make_async_copy(w_down.at[e], down_buf.at[slot], load_sem.at[2, slot]),
        )

    def loads(e, slot):
        return (load_x(e, slot, 0),) + load_w(e, slot) + (load_x(e, slot, 1),)

    for copy in loads(0, 0):
        copy.start()

    def greet(k, carry):
        pl.semaphore_signal(barrier, inc=1, device_id={"ep": (me + k) & (n - 1)}, device_id_type=MESH)
        return carry
    lax.fori_loop(1, n, greet, 0)

    beyond, before = needs(expert_t[...], slot_t[...], n * experts, experts)
    note[...] = jnp.zeros_like(note)
    note[0:experts, 0:sources] = fill_v[...].astype(F32)
    note[experts:experts + 1, :] = jnp.max(before + beyond, axis=0, keepdims=True)
    def own_copy(e):
        return pltpu.make_async_copy(rows.at[1, e], own.at[e], own_sem.at[e])

    def pair_copy(e):
        return pltpu.make_async_remote_copy(
            src_ref=rows.at[0, e], dst_ref=theirs.at[e], send_sem=pair_send.at[e], recv_sem=pair_recv.at[e],
            device_id={"ep": me + 1 - 2 * core}, device_id_type=MESH)

    def block(t, carry):
        e = lax.shift_right_logical(t, 1)
        h = t & 1
        slot = e & 1
        to_core = (core + 1 + h) & 1

        @pl.when((h == 0) & (e + 1 < experts))
        def _():
            for copy in loads(e + 1, 1 - slot):
                copy.start()

        for j in range(chips):
            mask[pl.ds(j * cap, cap), :] = one(iota((cap, 128), 0) < fill[e, 2 * j + to_core])
        weights = load_w(e, slot)
        load_x(e, slot, h).wait()

        @pl.when(h == 0)
        def _():
            weights[0].wait()
            weights[1].wait()

        def up(k, carry):
            cols = pl.ds(pl.multiple_of(k * COLS, COLS), COLS)
            act = x_buf[slot, h].reshape(chips * cap, width)
            a = jnp.dot(act, gate_buf[slot, :, cols], preferred_element_type=F32)
            b = jnp.dot(act, up_buf[slot, :, cols], preferred_element_type=F32)
            hidden[:, cols] = (a * jax.nn.sigmoid(a) * b).astype(BF16)
            return carry
        lax.fori_loop(0, ffn // COLS, up, 0, unroll=True)

        @pl.when(h == 0)
        def _():
            weights[2].wait()

        def down(k, carry):
            live = jnp.concatenate([mask[...]] * (COLS // 128), axis=1) > 0.5
            tops = []
            for part in range(2):
                cols = pl.ds(pl.multiple_of(part * half + k * COLS, COLS), COLS)
                y = jnp.dot(hidden[...], down_buf[slot, :, cols], preferred_element_type=F32)
                y = jnp.where(live, y, 0.0)
                rows[h, e, :, :, cols] = y.astype(BF16).reshape(chips, cap, COLS)
                tops.append(y.reshape(chips, cap, COLS)[:, :8])
            first = iota((chips, 8, COLS), 1) < HEAD
            shifted = pltpu.roll(tops[1], HEAD, 1)
            cols = pl.ds(pl.multiple_of(k * COLS, COLS), COLS)
            head[h, e, :, :, cols] = jnp.where(first, tops[0], shifted).astype(BF16)
            return carry
        lax.fori_loop(0, half // COLS, down, 0, unroll=True)

        @pl.when(t == 0)
        def _():
            pl.semaphore_wait(barrier, n - 1)

        def push(j):
            pltpu.make_async_remote_copy(
                src_ref=head.at[h, e, j], dst_ref=head_in.at[me * HEADED + e], send_sem=head_send.at[h],
                recv_sem=head_recv, device_id={"ep": 2 * j + to_core}, device_id_type=MESH).start()

        @pl.when(e < HEADED)
        def _():
            def away(i, carry):
                push(step_to(chip, side, i))
                return carry
            lax.fori_loop(0, chips - 1, away, 0)

        @pl.when((h == 0) & (e < HEADED))
        def _():
            push(chip)

        @pl.when((h == 1) & (e < HEADED))
        def _():
            pltpu.make_async_copy(head.at[1, e, chip], head_in.at[me * HEADED + e], head_recv).start()

        @pl.when(h == 0)
        def _():
            pair_copy(e).start()

        @pl.when(h == 1)
        def _():
            own_copy(e).start()

        @pl.when(t == 0)
        def _():
            def tell(k, carry):
                pltpu.make_async_remote_copy(
                    src_ref=note, dst_ref=table.at[me], send_sem=note_send, recv_sem=note_recv,
                    device_id={"ep": (me + k) & (n - 1)}, device_id_type=MESH).start()
                return carry
            lax.fori_loop(1, n, tell, 0)
            table[me] = note[...]
        return carry
    lax.fori_loop(0, 2 * experts, block, 0)

    noted = table.at[pl.ds(0, n - 1)]
    pltpu.make_async_copy(noted, noted, note_recv).wait()
    pltpu.make_async_copy(noted, noted, note_send).wait()
    place_rows(table, me, core, n, experts, cap, place)
    for e in range(experts):
        pair_copy(e).wait_recv()

    def chunk(j):
        lanes = 2 * experts * cap
        pick = one(iota((cut + rest, lanes), 0) == place[pl.ds(2 * j + core, 1), :]).astype(BF16)
        near = rows[1, :, pl.ds(j, 1)].reshape(experts * cap, width)
        far = theirs[:, pl.ds(j, 1)].reshape(experts * cap, width)
        both = jnp.concatenate([near, far], axis=0)
        return jnp.dot(pick, both, preferred_element_type=F32).astype(BF16)

    def send(p, i, j):
        return pltpu.make_async_remote_copy(
            src_ref=(pack_a, pack_b)[p].at[i], dst_ref=(got_a, got_b)[p].at[i], send_sem=send_sem.at[p],
            recv_sem=recv_sem.at[p], device_id={"ep": 2 * j + core}, device_id_type=MESH)

    def push_first(i, carry):
        j = step_to(chip, side, i)
        block = chunk(j)
        pack_a[i] = block[:cut]
        pack_b[i] = block[cut:]
        send(0, i, j).start()
        return carry
    lax.fori_loop(0, chips - 1, push_first, 0)

    def push_rest(i, carry):
        send(1, i, step_to(chip, side, i)).start()
        return carry
    lax.fori_loop(0, chips - 1, push_rest, 0)
    block = chunk(chip)
    got_a[chips - 1] = block[:cut]
    got_b[chips - 1] = block[cut:]

    theirs_copy = pltpu.make_async_copy(theirs, other, theirs_sem)
    theirs_copy.start()
    most = jnp.max(jnp.max(table[...], axis=0)[experts:experts + 1, :])
    index = (most > float(cut + rest)).astype(I32)
    for more in MORE:
        index = index + (most > float(cut + rest + more)).astype(I32)
    branch[0, 0] = index

    _, before = needs(expert_t[...], slot_t[...], n * experts, experts)
    head_spot, order, spot = token_spots(expert_t[...], slot_t[...], before, chip, side, experts)
    key_a = jnp.where((spot >= 0) & (spot < cut), order * cut + spot, -64)
    key_b = jnp.where((spot >= cut) & (spot < cut + rest), order * rest + spot - cut, -64)
    set_keys(keys, (head_spot, key_a, key_b), weight_t[...])
    mix(keys, top, 0, 3 * top, 0, head_mix.at[pl.ds(0, 3 * tokens)], 0)
    mix(keys, top, 0, 3 * top, HEAD, head_mix.at[pl.ds(3 * tokens, 3 * tokens)], 0)
    mix(keys, top, top, 3 * top, 0, mix_a, 0)
    mix(keys, top, 2 * top, 3 * top, 0, mix_b, 0)
    pltpu.make_async_copy(head_in, head_in, head_recv).wait()

    def head_cols(i, carry):
        cols = pl.ds(pl.multiple_of(i * COLS, COLS), COLS)
        head_rows = head_in.shape[0] * head_in.shape[1]
        v = jnp.dot(head_mix[...], head_in[:, :, cols].reshape(head_rows, COLS), preferred_element_type=F32)
        total[:, cols] = fold(v, 0, tokens)
        total[:, pl.ds(pl.multiple_of(half + i * COLS, COLS), COLS)] = fold(v, 3 * tokens, tokens)
        return carry
    lax.fori_loop(0, half // COLS, head_cols, 0)

    for p, (got, mix_ref) in enumerate(((got_a, mix_a), (got_b, mix_b))):
        taken = got.at[pl.ds(0, chips - 1)]
        pltpu.make_async_copy(taken, taken, recv_sem.at[p]).wait()

        def some_cols(i, carry):
            cols = pl.ds(pl.multiple_of(i * COLS, COLS), COLS)
            total[:, cols] += weigh(got, mix_ref, cols)
            return carry
        lax.fori_loop(0, width // COLS, some_cols, 0, unroll=p == 1)

    for p, sent in enumerate((pack_a, pack_b)):
        pltpu.make_async_copy(sent, sent, send_sem.at[p]).wait()
    for e in range(experts):
        own_copy(e).wait()
        pair_copy(e).wait_send()
    for h in range(2):
        sent = head.at[h, pl.ds(0, HEADED), pl.ds(0, chips - h)]
        pltpu.make_async_copy(sent, sent, head_send.at[h]).wait()
    theirs_copy.wait()


def split3(w):
    hi = jnp.minimum(w, 3.3895313892515355e38).astype(BF16)
    rest = w - hi.astype(F32)
    mid = rest.astype(BF16)
    low = (rest - mid.astype(F32)).astype(BF16)
    return hi, mid, low


def more_kernel(n, room, table, expert_t, slot_t, weight_t, total, own, other, out,
                src, pack, got, mix_ref, place, keys, load_sem, send_sem, recv_sem):
    me = lax.axis_index("ep")
    core = me & 1
    chip = lax.shift_right_logical(me, 1)
    chips = n // 2
    side = math.isqrt(chips)
    experts, _, cap, width = own.shape
    top, tokens = expert_t.shape
    barrier = pltpu.get_barrier_semaphore()

    def greet(i, carry):
        pl.semaphore_signal(barrier, inc=1, device_id={"ep": 2 * step_to(chip, side, i) + core}, device_id_type=MESH)
        return carry
    lax.fori_loop(0, chips - 1, greet, 0)

    def load(i, j):
        return (pltpu.make_async_copy(own.at[:, j], src.at[i, 0], load_sem.at[i, 0]),
                pltpu.make_async_copy(other.at[:, j], src.at[i, 1], load_sem.at[i, 1]))

    def load_to(i, carry):
        for copy in load(i, step_to(chip, side, i)):
            copy.start()
        return carry
    lax.fori_loop(0, chips - 1, load_to, 0)
    for copy in load(chips - 1, chip):
        copy.start()
    place_rows(table, me, core, n, experts, cap, place)

    def chunk(i, j):
        for copy in load(i, j):
            copy.wait()
        lanes = 2 * experts * cap
        pick = one(iota((room, lanes), 0) + ROOM == place[pl.ds(2 * j + core, 1), :]).astype(BF16)
        return jnp.dot(pick, src[i].reshape(lanes, width), preferred_element_type=F32).astype(BF16)

    def send(i, j):
        return pltpu.make_async_remote_copy(
            src_ref=pack.at[i], dst_ref=got.at[i], send_sem=send_sem, recv_sem=recv_sem,
            device_id={"ep": 2 * j + core}, device_id_type=MESH)

    pl.semaphore_wait(barrier, chips - 1)

    def push(i, carry):
        j = step_to(chip, side, i)
        pack[i] = chunk(i, j)
        send(i, j).start()
        return carry
    lax.fori_loop(0, chips - 1, push, 0)
    got[chips - 1] = chunk(chips - 1, chip)

    _, before = needs(expert_t[...], slot_t[...], n * experts, experts)
    _, order, spot = token_spots(expert_t[...], slot_t[...], before, chip, side, experts)
    key = jnp.where((spot >= ROOM) & (spot < ROOM + room), order * room + spot - ROOM, -64)
    set_keys(keys, (key,), weight_t[...])
    mix(keys, top, 0, top, 0, mix_ref, 0)

    taken = got.at[pl.ds(0, chips - 1)]
    pltpu.make_async_copy(taken, taken, recv_sem).wait()

    def cols_of(i, carry):
        cols = pl.ds(pl.multiple_of(i * COLS, COLS), COLS)
        out[:, cols] = total[:, cols] + weigh(got, mix_ref, cols)
        return carry
    lax.fori_loop(0, width // COLS, cols_of, 0)
    pltpu.make_async_copy(pack, pack, send_sem).wait()


def solution(mesh):
    n = mesh.shape["ep"]
    chips = n // 2

    def step(dispatched, w_gate, w_up, w_down, fill_count, slot_index, expert_id, gate_weight):
        sources, experts, cap, width = dispatched.shape
        ffn = w_gate.shape[2]
        tokens, top = slot_index.shape
        most = 2 * (HEADED * (cap - HEAD) + (experts - HEADED) * cap)
        cut = -(-ROOM // 16) * 8
        any_spec = pl.BlockSpec(memory_space=pl.ANY)
        vmem_spec = pl.BlockSpec(memory_space=pltpu.VMEM)
        smem_spec = pl.BlockSpec(memory_space=pltpu.SMEM)
        shape = jax.ShapeDtypeStruct
        vmem = pltpu.VMEM
        dma = pltpu.SemaphoreType.DMA
        fill_t, expert_t, slot_t, weight_t = fill_count.T, expert_id.T, slot_index.T, gate_weight.T
        own, other, table, branch, total = pl.pallas_call(
            functools.partial(main_kernel, n),
            name="main",
            out_shape=(
                shape((experts, chips, cap, width), BF16),
                shape((experts, chips, cap, width), BF16),
                shape((n, 8, 128), F32),
                shape((1, 1), I32),
                shape((tokens, width), F32),
            ),
            in_specs=[smem_spec] + [vmem_spec] * 4 + [any_spec] * 4,
            out_specs=(any_spec,) * 2 + (vmem_spec, smem_spec, vmem_spec),
            scratch_shapes=[
                vmem((2, 2, chips, cap, width), BF16),
                vmem((2, width, ffn), BF16),
                vmem((2, width, ffn), BF16),
                vmem((2, ffn, width), BF16),
                vmem((chips * cap, ffn), BF16),
                vmem((chips * cap, 128), F32),
                vmem((2, experts, chips, cap, width), BF16),
                vmem((experts, chips, cap, width), BF16),
                vmem((2, experts, chips, 8, width // 2), BF16),
                vmem((n * HEADED, 8, width // 2), BF16),
                vmem((8, 128), F32),
                vmem((n, 2 * experts * cap), I32),
                vmem((tokens, 128), F32),
                vmem((6 * tokens, n * HEADED * 8), BF16),
                vmem((3 * tokens, chips * cut), BF16),
                vmem((3 * tokens, chips * (ROOM - cut)), BF16),
                vmem((chips - 1, cut, width), BF16),
                vmem((chips - 1, ROOM - cut, width), BF16),
                vmem((chips, cut, width), BF16),
                vmem((chips, ROOM - cut, width), BF16),
                dma((3, 2)), dma((2, 2)), dma((experts,)), dma, dma((experts,)), dma((experts,)), dma((2,)), dma, dma, dma, dma((2,)), dma((2,)),
            ],
            compiler_params=pltpu.CompilerParams(collective_id=0, has_side_effects=True, vmem_limit_bytes=GRANT),
        )(fill_t, fill_t, expert_t, slot_t, weight_t, dispatched.reshape(chips, 2, experts, cap, width), w_gate, w_up, w_down)

        def more(room, index):
            result = pl.pallas_call(
                functools.partial(more_kernel, n, room),
                name="more%d" % room,
                out_shape=shape((tokens, width), F32),
                in_specs=[vmem_spec] * 5 + [any_spec] * 2,
                out_specs=vmem_spec,
                scratch_shapes=[
                    vmem((chips, 2, experts, cap, width), BF16),
                    vmem((chips - 1, room, width), BF16),
                    vmem((chips, room, width), BF16),
                    vmem((3 * tokens, chips * room), BF16),
                    vmem((n, 2 * experts * cap), I32),
                    vmem((tokens, 128), F32),
                    dma((chips, 2)), dma, dma,
                ],
                compiler_params=pltpu.CompilerParams(collective_id=1 + index, has_side_effects=True, vmem_limit_bytes=GRANT),
            )(table, expert_t, slot_t, weight_t, total, own, other)
            return result.astype(BF16)

        rooms = MORE + (most - ROOM,)
        return lax.switch(branch[0, 0], [lambda: total.astype(BF16)] + [functools.partial(more, r, i) for i, r in enumerate(rooms)])

    token_spec = P(("dp", "ep"))
    in_specs = (P("dp", "ep"), P("ep"), P("ep"), P("ep"), P("dp", "ep"), token_spec, token_spec, token_spec)
    return jax.shard_map(step, mesh=mesh, in_specs=in_specs, out_specs=token_spec, check_vma=False)
```

time: 186 us -> 78.8 us (0.42)
  the two profiles are of different devices: /device:TPU:103 before, /device:TPU:96 now
where the time goes in v1:
time: 78.8 us; the launch traced here: 78.7 us
  Pallas kernels  75.9 us (96%)
  other arithmetic  2.09 us (3%)
    pallas_call x1, Pallas kernels, step(): pl.pallas_call(functools.partial(main_kernel, n), name='main', out_shape=...  75.9 us
    convert_element_type x1, other arithmetic, step(): total.astype(BF16)  2.09 us

profile of v1, /device:TPU:96, one launch (start us, length us, event | category | flops | bytes accessed | tf_op | source)
XLA Modules:
  0.0 78.7 jit_solution(15537904975952315332)
XLA Ops:
  0.0 75.9 %main.1 = (bf16[4,16,16,2048]{3,2,1,0:T(8,128)(2,1)}, bf16[4,16,16,2048]{3,2,1,0:T(8,128)(2,1)}, f32[32,8,128]{2,1,0:T(8,128)}, s32[1,1]{1,0:T(1,128)}, f32[128,2048]{1,0:T(8,128)}) custom-call(s32[4,32]{1,0:T(4,128)} %bitcast.25, s32[4,32]{1,0:T(4,128)} %bitcast.26, s32[8,128]{1,0:T(8,128)} %bitcast.7, s32[8,128]{1,0:T(8,128)} %bitcast.13, ...), custom_call_target="tpu_custom_call" | custom-call | tf_op jit(solution)/shard_map/main/pallas_call | solution.py:447
  76.6 2.1 %convert_element_type.32 = bf16[128,2048]{1,0:T(8,128)(2,1)} convert(f32[128,2048]{1,0:T(8,128)} %get-tuple-element.138) | non-fusion elementwise | flops 262144 | bytes 1572864 | tf_op jit(solution)/shard_map/cond/branch_0_fun/convert_element_type | solution.py:506
  (1 shorter events, 0.0 us)

commit v2 on v1

--- a/solution.py
+++ b/solution.py
@@ -13,6 +13,7 @@
 HEAD = 4
 HEADED = 3
 COLS = 256
+UNROLL = 3
 ROOM = 48
 MORE = (8, 16, 24, 40)
 GRANT = 64 * 1024 * 1024 - 65536
@@ -31,6 +32,14 @@
     return lax.broadcasted_iota(I32, shape, dim)
 
 
+def low(v, m):
+    return v & (m - 1)
+
+
+def high(v, m):
+    return lax.shift_right_logical(v, m.bit_length() - 1)
+
+
 def one(cond):
     return jnp.where(cond, 1.0, 0.0)
 
@@ -41,10 +50,10 @@
     for c in range(expert_t.shape[0]):
         hit = hit + one((iota((total, tokens), 0) == expert_t[c:c + 1]) & (slot_t[c:c + 1] >= 0))
     count = jnp.sum(hit, axis=1, keepdims=True)
-    headed = lax.rem(iota((total, 1), 0), experts) < HEADED
+    headed = low(iota((total, 1), 0), experts) < HEADED
     beyond = jnp.maximum(count - jnp.where(headed, float(HEAD), 0.0), 0.0)
     g, p = iota((total, total), 0), iota((total, total), 1)
-    lower = one((g // (2 * experts) == p // (2 * experts)) & (p < g)).astype(BF16)
+    lower = one((high(g, 2 * experts) == high(p, 2 * experts)) & (p < g)).astype(BF16)
     before = jnp.dot(lower, jnp.broadcast_to(beyond, (total, 128)).astype(BF16), preferred_element_type=F32)
     return beyond, before
 
@@ -54,16 +63,16 @@
     fills = jnp.concatenate([table[me, 0:experts], table[me + 1 - 2 * core, 0:experts], jnp.zeros((128 - 2 * experts, 128), F32)])
     fills = fills.T
     k, lane = iota((128, lanes), 0), iota((128, lanes), 1)
-    early = lax.rem(iota((128, 128), 1), experts) < HEADED
+    early = low(iota((128, 128), 1), experts) < HEADED
     extra = jnp.maximum(fills - jnp.where(early, float(HEAD), 0.0), 0.0)
-    rank_k = lax.rem(k + experts * core, 2 * experts)
-    rank_l = lax.rem(lane // cap + experts * core, 2 * experts)
-    spread = one(k == lane // cap).astype(BF16)
+    rank_k = low(k + experts * core, 2 * experts)
+    rank_l = low(high(lane, cap) + experts * core, 2 * experts)
+    spread = one(k == high(lane, cap)).astype(BF16)
     earlier = one((rank_k < rank_l) & (k < 2 * experts)).astype(BF16)
     filled = jnp.dot(fills.astype(BF16), spread, preferred_element_type=F32)
     start = jnp.dot(extra.astype(BF16), earlier, preferred_element_type=F32)
-    slot = lax.rem(lane, cap)
-    skip = jnp.where(lax.rem(lane // cap, experts) < HEADED, HEAD, 0)
+    slot = low(lane, cap)
+    skip = jnp.where(low(high(lane, cap), experts) < HEADED, HEAD, 0)
     spot = jnp.where((slot >= skip) & (slot.astype(F32) < filled), start.astype(I32) + slot - skip, -1)
     place[...] = spot[0:n]
 
@@ -75,11 +84,11 @@
         hit = iota((total, tokens), 0) == expert[c:c + 1]
         lead.append(jnp.sum(jnp.where(hit, before, 0.0), axis=0, keepdims=True))
     lead = jnp.concatenate(lead, axis=0).astype(I32)
-    local = lax.rem(expert, experts)
+    local = low(expert, experts)
     early = local < HEADED
     in_head = early & (slot >= 0) & (slot < HEAD)
-    head_spot = jnp.where(in_head, ((expert // experts) * HEADED + local) * 8 + slot, -64)
-    home = expert // (2 * experts)
+    head_spot = jnp.where(in_head, (high(expert, experts) * HEADED + local) * 8 + slot, -64)
+    home = high(expert, 2 * experts)
     order = jnp.full(expert.shape, side * side - 1, I32)
     for i, (dx, dy) in enumerate(ORDER):
         came = lax.rem(chip // side + side - dy, side) * side + lax.rem(lax.rem(chip, side) + side - dx, side)
@@ -121,9 +130,9 @@
 
 
 def main_kernel(n, fill, fill_v, expert_t, slot_t, weight_t, x, w_gate, w_up, w_down, own, other, table, branch, total,
-                x_buf, gate_buf, up_buf, down_buf, hidden, mask, rows, theirs, head, head_in, note, place, keys,
+                x_buf, gate_buf, up_buf, down_buf, hidden_a, hidden_b, mask, rows, theirs, head, head_in, note, place, keys,
                 head_mix, mix_a, mix_b, pack_a, pack_b, got_a, got_b,
-                load_sem, x_sem, own_sem, theirs_sem, pair_send, pair_recv, head_send, head_recv, note_send, note_recv, send_sem, recv_sem):
+                load_sem, x_sem, piece_sem, own_sem, theirs_sem, pair_send, pair_recv, head_send, head_recv, note_send, note_recv, send_sem, recv_sem):
     me = lax.axis_index("ep")
     core = me & 1
     chip = lax.shift_right_logical(me, 1)
@@ -136,33 +145,48 @@
     top, tokens = expert_t.shape
     cut = got_a.shape[1]
     rest = got_b.shape[1]
+    hidden = (hidden_a, hidden_b)
     barrier = pltpu.get_barrier_semaphore()
 
-    def load_x(e, slot, h):
-        return pltpu.make_async_copy(x.at[:, (core + 1 + h) & 1, e], x_buf.at[slot, h], x_sem.at[slot, h])
-
-    def load_w(e, slot):
-        return (
-            pltpu.make_async_copy(w_gate.at[e], gate_buf.at[slot], load_sem.at[0, slot]),
-            pltpu.make_async_copy(w_up.at[e], up_buf.at[slot], load_sem.at[1, slot]),
-            pltpu.make_async_copy(w_down.at[e], down_buf.at[slot], load_sem.at[2, slot]),
-        )
-
-    def loads(e, slot):
-        return (load_x(e, slot, 0),) + load_w(e, slot) + (load_x(e, slot, 1),)
-
-    for copy in loads(0, 0):
-        copy.start()
+    def load_x(e, h):
+        return pltpu.make_async_copy(x.at[:, (core + 1 + h) & 1, e], x_buf.at[e & 1, h], x_sem.at[e & 1, h])
+
+    def load_in(e):
+        return (pltpu.make_async_copy(w_gate.at[e], gate_buf.at[e & 1], load_sem.at[0, e & 1]),
+                pltpu.make_async_copy(w_up.at[e], up_buf.at[e & 1], load_sem.at[1, e & 1]))
+
+    def load_down(e):
+        return pltpu.make_async_copy(w_down.at[e], down_buf.at[e & 1], load_sem.at[2, e & 1])
+
+    def load_piece(k):
+        cols = pl.ds(k * COLS, COLS)
+        return (pltpu.make_async_copy(w_gate.at[0, :, cols], gate_buf.at[0, :, cols], piece_sem.at[0, k]),
+                pltpu.make_async_copy(w_up.at[0, :, cols], up_buf.at[0, :, cols], piece_sem.at[1, k]))
+
+    pieces = ffn // COLS
+    load_x(0, 0).start()
+    for k in range(pieces):
+        for copy in load_piece(k):
+            copy.start()
+    load_down(0).start()
+    load_x(0, 1).start()
 
     def greet(k, carry):
         pl.semaphore_signal(barrier, inc=1, device_id={"ep": (me + k) & (n - 1)}, device_id_type=MESH)
         return carry
-    lax.fori_loop(1, n, greet, 0)
+    lax.fori_loop(1, n, greet, 0, unroll=8)
 
     beyond, before = needs(expert_t[...], slot_t[...], n * experts, experts)
     note[...] = jnp.zeros_like(note)
     note[0:experts, 0:sources] = fill_v[...].astype(F32)
     note[experts:experts + 1, :] = jnp.max(before + beyond, axis=0, keepdims=True)
+    def set_mask(t, carry):
+        for j in range(chips):
+            full = fill[lax.shift_right_logical(t, 1), 2 * j + ((core + 1 + t) & 1)]
+            mask[t, pl.ds(j * cap, cap), :] = one(iota((cap, 128), 0) < full)
+        return carry
+    lax.fori_loop(0, 2 * experts, set_mask, 0)
+
     def own_copy(e):
         return pltpu.make_async_copy(rows.at[1, e], own.at[e], own_sem.at[e])
 
@@ -171,99 +195,112 @@
             src_ref=rows.at[0, e], dst_ref=theirs.at[e], send_sem=pair_send.at[e], recv_sem=pair_recv.at[e],
             device_id={"ep": me + 1 - 2 * core}, device_id_type=MESH)
 
-    def block(t, carry):
-        e = lax.shift_right_logical(t, 1)
-        h = t & 1
-        slot = e & 1
-        to_core = (core + 1 + h) & 1
-
-        @pl.when((h == 0) & (e + 1 < experts))
-        def _():
-            for copy in loads(e + 1, 1 - slot):
+    def up(e, h, k):
+        cols = pl.ds(k * COLS, COLS)
+        act = x_buf[e & 1, h].reshape(chips * cap, width)
+        a = jnp.dot(act, gate_buf[e & 1, :, cols], preferred_element_type=F32)
+        b = jnp.dot(act, up_buf[e & 1, :, cols], preferred_element_type=F32)
+        hidden[h][:, cols] = (a * jax.nn.sigmoid(a) * b).astype(BF16)
+
+    def down(e, h, k):
+        live = jnp.concatenate([mask[2 * e + h]] * (COLS // 128), axis=1) > 0.5
+        tops = []
+        for part in range(2):
+            cols = pl.ds(part * half + k * COLS, COLS)
+            y = jnp.dot(hidden[h][...], down_buf[e & 1, :, cols], preferred_element_type=F32)
+            y = jnp.where(live, y, 0.0)
+            rows[h, e, :, :, cols] = y.astype(BF16).reshape(chips, cap, COLS)
+            tops.append(y.reshape(chips, cap, COLS)[:, :8])
+        first = iota((chips, 8, COLS), 1) < HEAD
+        shifted = pltpu.roll(tops[1], HEAD, 1)
+        head[h, e, :, :, pl.ds(k * COLS, COLS)] = jnp.where(first, tops[0], shifted).astype(BF16)
+
+    outs = half // COLS
+
+    def both(e_up, h_up, e_down, h_down):
+        for k in range(max(pieces, outs)):
+            if k < pieces:
+                up(e_up, h_up, k)
+            if k < outs:
+                down(e_down, h_down, k)
+
+    def push(e, h, j):
+        pltpu.make_async_remote_copy(
+            src_ref=head.at[h, e, j], dst_ref=head_in.at[me * HEADED + e], send_sem=head_send.at[h],
+            recv_sem=head_recv, device_id={"ep": 2 * j + ((core + 1 + h) & 1)}, device_id_type=MESH).start()
+
+    def push_all(e, h):
+        def away(i, carry):
+            push(e, h, step_to(chip, side, i))
+            return carry
+        lax.fori_loop(0, chips - 1, away, 0, unroll=True)
+
+    load_x(0, 0).wait()
+    for k in range(pieces):
+        for copy in load_piece(k):
+            copy.wait()
+        if k == pieces - 1:
+            for copy in load_in(1) + (load_x(1, 0), load_x(1, 1), load_down(1)):
                 copy.start()
-
-        for j in range(chips):
-            mask[pl.ds(j * cap, cap), :] = one(iota((cap, 128), 0) < fill[e, 2 * j + to_core])
-        weights = load_w(e, slot)
-        load_x(e, slot, h).wait()
-
-        @pl.when(h == 0)
-        def _():
-            weights[0].wait()
-            weights[1].wait()
-
-        def up(k, carry):
-            cols = pl.ds(pl.multiple_of(k * COLS, COLS), COLS)
-            act = x_buf[slot, h].reshape(chips * cap, width)
-            a = jnp.dot(act, gate_buf[slot, :, cols], preferred_element_type=F32)
-            b = jnp.dot(act, up_buf[slot, :, cols], preferred_element_type=F32)
-            hidden[:, cols] = (a * jax.nn.sigmoid(a) * b).astype(BF16)
-            return carry
-        lax.fori_loop(0, ffn // COLS, up, 0, unroll=True)
-
-        @pl.when(h == 0)
-        def _():
-            weights[2].wait()
-
-        def down(k, carry):
-            live = jnp.concatenate([mask[...]] * (COLS // 128), axis=1) > 0.5
-            tops = []
-            for part in range(2):
-                cols = pl.ds(pl.multiple_of(part * half + k * COLS, COLS), COLS)
-                y = jnp.dot(hidden[...], down_buf[slot, :, cols], preferred_element_type=F32)
-                y = jnp.where(live, y, 0.0)
-                rows[h, e, :, :, cols] = y.astype(BF16).reshape(chips, cap, COLS)
-                tops.append(y.reshape(chips, cap, COLS)[:, :8])
-            first = iota((chips, 8, COLS), 1) < HEAD
-            shifted = pltpu.roll(tops[1], HEAD, 1)
-            cols = pl.ds(pl.multiple_of(k * COLS, COLS), COLS)
-            head[h, e, :, :, cols] = jnp.where(first, tops[0], shifted).astype(BF16)
-            return carry
-        lax.fori_loop(0, half // COLS, down, 0, unroll=True)
-
-        @pl.when(t == 0)
+        up(0, 0, k)
+
+    def expert(e, carry):
+        @pl.when((e > 0) & (e + 1 < experts))
+        def _():
+            load_down(e + 1).start()
+
+        load_x(e, 1).wait()
+        load_down(e).wait()
+        for k in range(outs):
+            down(e, 0, k)
+
+        @pl.when(e == 0)
         def _():
             pl.semaphore_wait(barrier, n - 1)
 
-        def push(j):
-            pltpu.make_async_remote_copy(
-                src_ref=head.at[h, e, j], dst_ref=head_in.at[me * HEADED + e], send_sem=head_send.at[h],
-                recv_sem=head_recv, device_id={"ep": 2 * j + to_core}, device_id_type=MESH).start()
+        pair_copy(e).start()
 
         @pl.when(e < HEADED)
         def _():
-            def away(i, carry):
-                push(step_to(chip, side, i))
-                return carry
-            lax.fori_loop(0, chips - 1, away, 0)
-
-        @pl.when((h == 0) & (e < HEADED))
-        def _():
-            push(chip)
-
-        @pl.when((h == 1) & (e < HEADED))
-        def _():
-            pltpu.make_async_copy(head.at[1, e, chip], head_in.at[me * HEADED + e], head_recv).start()
-
-        @pl.when(h == 0)
-        def _():
-            pair_copy(e).start()
-
-        @pl.when(h == 1)
-        def _():
-            own_copy(e).start()
-
-        @pl.when(t == 0)
+            push_all(e, 0)
+            push(e, 0, chip)
+
+        @pl.when(e == 0)
         def _():
             def tell(k, carry):
                 pltpu.make_async_remote_copy(
                     src_ref=note, dst_ref=table.at[me], send_sem=note_send, recv_sem=note_recv,
                     device_id={"ep": (me + k) & (n - 1)}, device_id_type=MESH).start()
                 return carry
-            lax.fori_loop(1, n, tell, 0)
+            lax.fori_loop(1, n, tell, 0, unroll=8)
             table[me] = note[...]
-        return carry
-    lax.fori_loop(0, 2 * experts, block, 0)
+
+        for k in range(pieces):
+            up(e, 1, k)
+
+        @pl.when(e + 2 < experts)
+        def _():
+            for copy in load_in(e + 2) + (load_x(e + 2, 0), load_x(e + 2, 1)):
+                copy.start()
+
+        for k in range(outs):
+            down(e, 1, k)
+        own_copy(e).start()
+
+        @pl.when(e < HEADED)
+        def _():
+            push_all(e, 1)
+            pltpu.make_async_copy(head.at[1, e, chip], head_in.at[me * HEADED + e], head_recv).start()
+
+        @pl.when(e + 1 < experts)
+        def _():
+            load_x(e + 1, 0).wait()
+            for copy in load_in(e + 1):
+                copy.wait()
+            for k in range(pieces):
+                up(e + 1, 0, k)
+        return carry
+    lax.fori_loop(0, experts, expert, 0)
 
     noted = table.at[pl.ds(0, n - 1)]
     pltpu.make_async_copy(noted, noted, note_recv).wait()
@@ -292,7 +329,7 @@
         pack_b[i] = block[cut:]
         send(0, i, j).start()
         return carry
-    lax.fori_loop(0, chips - 1, push_first, 0)
+    lax.fori_loop(0, chips - 1, push_first, 0, unroll=UNROLL)
 
     def push_rest(i, carry):
         send(1, i, step_to(chip, side, i)).start()
@@ -462,7 +499,8 @@
                 vmem((2, width, ffn), BF16),
                 vmem((2, ffn, width), BF16),
                 vmem((chips * cap, ffn), BF16),
-                vmem((chips * cap, 128), F32),
+                vmem((chips * cap, ffn), BF16),
+                vmem((2 * experts, chips * cap, 128), F32),
                 vmem((2, experts, chips, cap, width), BF16),
                 vmem((experts, chips, cap, width), BF16),
                 vmem((2, experts, chips, 8, width // 2), BF16),
@@ -477,7 +515,7 @@
                 vmem((chips - 1, ROOM - cut, width), BF16),
                 vmem((chips, cut, width), BF16),
                 vmem((chips, ROOM - cut, width), BF16),
-                dma((3, 2)), dma((2, 2)), dma((experts,)), dma, dma((experts,)), dma((experts,)), dma((2,)), dma, dma, dma, dma((2,)), dma((2,)),
+                dma((3, 2)), dma((2, 2)), dma((2, ffn // COLS)), dma((experts,)), dma, dma((experts,)), dma((experts,)), dma((2,)), dma, dma, dma, dma((2,)), dma((2,)),
             ],
             compiler_params=pltpu.CompilerParams(collective_id=0, has_side_effects=True, vmem_limit_bytes=GRANT),
         )(fill_t, fill_t, expert_t, slot_t, weight_t, dispatched.reshape(chips, 2, experts, cap, width), w_gate, w_up, w_down)

time: 78.8 us -> 76.8 us (0.975)
  Pallas kernels: 75.9 us -> 73.7 us
    pallas_call x1, Pallas kernels: 75.9 us -> 73.7 us  [step(): pl.pallas_call(functools.partial(main_kernel, n), name='main', out_shape=...]
where the time goes in v2:
time: 76.8 us; the launch traced here: 76.7 us
  Pallas kernels  73.7 us (96%)
  other arithmetic  2.09 us (3%)
    pallas_call x1, Pallas kernels, step(): pl.pallas_call(functools.partial(main_kernel, n), name='main', out_shape=...  73.7 us
    convert_element_type x1, other arithmetic, step(): total.astype(BF16)  2.09 us

profile of v2, /device:TPU:96, one launch (start us, length us, event | category | flops | bytes accessed | tf_op | source)
XLA Modules:
  0.0 76.7 jit_solution(16410618861447866010)
XLA Ops:
  0.0 73.7 %main.1 = (bf16[4,16,16,2048]{3,2,1,0:T(8,128)(2,1)}, bf16[4,16,16,2048]{3,2,1,0:T(8,128)(2,1)}, f32[32,8,128]{2,1,0:T(8,128)}, s32[1,1]{1,0:T(1,128)}, f32[128,2048]{1,0:T(8,128)}) custom-call(s32[4,32]{1,0:T(4,128)} %bitcast.25, s32[4,32]{1,0:T(4,128)} %bitcast.26, s32[8,128]{1,0:T(8,128)} %bitcast.7, s32[8,128]{1,0:T(8,128)} %bitcast.13, ...), custom_call_target="tpu_custom_call" | custom-call | tf_op jit(solution)/shard_map/main/pallas_call | solution.py:484
  74.4 0.2 conditional.4
  74.6 2.1 %convert_element_type.32 = bf16[128,2048]{1,0:T(8,128)(2,1)} convert(f32[128,2048]{1,0:T(8,128)} %get-tuple-element.138) | non-fusion elementwise | flops 262144 | bytes 1572864 | tf_op jit(solution)/shard_map/cond/branch_0_fun/convert_element_type | solution.py:544

commit v3 on v2

--- a/solution.py
+++ b/solution.py
@@ -14,6 +14,7 @@
 HEADED = 3
 COLS = 256
 UNROLL = 3
+CUT = 16
 ROOM = 48
 MORE = (8, 16, 24, 40)
 GRANT = 64 * 1024 * 1024 - 65536
@@ -53,8 +54,14 @@
     headed = low(iota((total, 1), 0), experts) < HEADED
     beyond = jnp.maximum(count - jnp.where(headed, float(HEAD), 0.0), 0.0)
     g, p = iota((total, total), 0), iota((total, total), 1)
-    lower = one((high(g, 2 * experts) == high(p, 2 * experts)) & (p < g)).astype(BF16)
-    before = jnp.dot(lower, jnp.broadcast_to(beyond, (total, 128)).astype(BF16), preferred_element_type=F32)
+    chip = high(g, 2 * experts) == high(p, 2 * experts)
+    late_g, late_p = low(g, experts) == experts - 1, low(p, experts) == experts - 1
+    first = one(chip & ~late_p & (late_g | (p < g))).astype(BF16)
+    last = one(chip & late_p & late_g & (p < g)).astype(BF16)
+    wide = jnp.broadcast_to(beyond, (total, 128)).astype(BF16)
+    before = jnp.dot(first, wide, preferred_element_type=F32)
+    late = low(iota((total, 128), 0), experts) == experts - 1
+    before = jnp.where(late, jnp.maximum(before, float(CUT)), before) + jnp.dot(last, wide, preferred_element_type=F32)
     return beyond, before
 
 
@@ -65,14 +72,20 @@
     k, lane = iota((128, lanes), 0), iota((128, lanes), 1)
     early = low(iota((128, 128), 1), experts) < HEADED
     extra = jnp.maximum(fills - jnp.where(early, float(HEAD), 0.0), 0.0)
+    k_lane = low(high(lane, cap), 2) * experts + high(lane, 2 * cap)
     rank_k = low(k + experts * core, 2 * experts)
-    rank_l = low(high(lane, cap) + experts * core, 2 * experts)
-    spread = one(k == high(lane, cap)).astype(BF16)
-    earlier = one((rank_k < rank_l) & (k < 2 * experts)).astype(BF16)
+    rank_l = low(k_lane + experts * core, 2 * experts)
+    late_k, late_l = low(k, experts) == experts - 1, low(k_lane, experts) == experts - 1
+    used = k < 2 * experts
+    spread = one(k == k_lane).astype(BF16)
+    first = one(used & ~late_k & (late_l | (rank_k < rank_l))).astype(BF16)
+    last = one(used & late_k & late_l & (rank_k < rank_l)).astype(BF16)
     filled = jnp.dot(fills.astype(BF16), spread, preferred_element_type=F32)
-    start = jnp.dot(extra.astype(BF16), earlier, preferred_element_type=F32)
+    start = jnp.dot(extra.astype(BF16), first, preferred_element_type=F32)
+    start = jnp.where(late_l, jnp.maximum(start, float(CUT)), start)
+    start = start + jnp.dot(extra.astype(BF16), last, preferred_element_type=F32)
     slot = low(lane, cap)
-    skip = jnp.where(low(high(lane, cap), experts) < HEADED, HEAD, 0)
+    skip = jnp.where(low(k_lane, experts) < HEADED, HEAD, 0)
     spot = jnp.where((slot >= skip) & (slot.astype(F32) < filled), start.astype(I32) + slot - skip, -1)
     place[...] = spot[0:n]
 
@@ -129,8 +142,8 @@
     return fold(v, 0, mix_ref.shape[0] // 3)
 
 
-def main_kernel(n, fill, fill_v, expert_t, slot_t, weight_t, x, w_gate, w_up, w_down, own, other, table, branch, total,
-                x_buf, gate_buf, up_buf, down_buf, hidden_a, hidden_b, mask, rows, theirs, head, head_in, note, place, keys,
+def main_kernel(n, fill_in, expert_in, slot_in, weight_in, x, w_gate, w_up, w_down, own, other, table, branch, total_out,
+                fill, fill_v, expert_t, slot_t, weight_t, total, small_sem, out_sem, x_buf, gate_buf, up_buf, down_buf, hidden_a, hidden_b, mask, rows, theirs, head, head_in, note, place, keys,
                 head_mix, mix_a, mix_b, pack_a, pack_b, got_a, got_b,
                 load_sem, x_sem, piece_sem, own_sem, theirs_sem, pair_send, pair_recv, head_send, head_recv, note_send, note_recv, send_sem, recv_sem):
     me = lax.axis_index("ep")
@@ -164,8 +177,14 @@
                 pltpu.make_async_copy(w_up.at[0, :, cols], up_buf.at[0, :, cols], piece_sem.at[1, k]))
 
     pieces = ffn // COLS
+    smalls = [pltpu.make_async_copy(a, b, small_sem.at[i]) for i, (a, b) in enumerate((
+        (fill_in, fill), (fill_in, fill_v), (expert_in, expert_t), (slot_in, slot_t), (weight_in, weight_t)))]
     load_x(0, 0).start()
-    for k in range(pieces):
+    for copy in load_piece(0):
+        copy.start()
+    for copy in smalls:
+        copy.start()
+    for k in range(1, pieces):
         for copy in load_piece(k):
             copy.start()
     load_down(0).start()
@@ -176,6 +195,8 @@
         return carry
     lax.fori_loop(1, n, greet, 0, unroll=8)
 
+    for copy in smalls:
+        copy.wait()
     beyond, before = needs(expert_t[...], slot_t[...], n * experts, experts)
     note[...] = jnp.zeros_like(note)
     note[0:experts, 0:sources] = fill_v[...].astype(F32)
@@ -235,6 +256,34 @@
             return carry
         lax.fori_loop(0, chips - 1, away, 0, unroll=True)
 
+    def wait_notes(sem):
+        noted = table.at[pl.ds(0, n - 1)]
+        pltpu.make_async_copy(noted, noted, sem).wait()
+
+    def chunk(p, j, count):
+        first, size = ((0, cut), (cut, rest))[p]
+        lanes = 2 * count * cap
+        spots = place[pl.ds(2 * j + core, 1), :]
+        pick = one(iota((size, lanes), 0) + first == spots[:, :lanes]).astype(BF16)
+        near = rows[1, 0:count, pl.ds(j, 1)]
+        far = theirs[0:count, pl.ds(j, 1)]
+        source = jnp.concatenate([near, far], axis=1).reshape(lanes, width)
+        return jnp.dot(pick, source, preferred_element_type=F32).astype(BF16)
+
+    def send(p, i, j):
+        return pltpu.make_async_remote_copy(
+            src_ref=(pack_a, pack_b)[p].at[i], dst_ref=(got_a, got_b)[p].at[i], send_sem=send_sem.at[p],
+            recv_sem=recv_sem.at[p], device_id={"ep": 2 * j + core}, device_id_type=MESH)
+
+    def push_block(p, count):
+        def one_chip(i, carry):
+            j = step_to(chip, side, i)
+            (pack_a, pack_b)[p][i] = chunk(p, j, count)
+            send(p, i, j).start()
+            return carry
+        lax.fori_loop(0, chips - 1, one_chip, 0, unroll=UNROLL)
+        (got_a, got_b)[p][chips - 1] = chunk(p, chip, count)
+
     load_x(0, 0).wait()
     for k in range(pieces):
         for copy in load_piece(k):
@@ -292,6 +341,14 @@
             push_all(e, 1)
             pltpu.make_async_copy(head.at[1, e, chip], head_in.at[me * HEADED + e], head_recv).start()
 
+        @pl.when(e == experts - 2)
+        def _():
+            wait_notes(note_recv)
+            place_rows(table, me, core, n, experts, cap, place)
+            for done in range(experts - 1):
+                pair_copy(done).wait_recv()
+            push_block(0, experts - 1)
+
         @pl.when(e + 1 < experts)
         def _():
             load_x(e + 1, 0).wait()
@@ -302,42 +359,9 @@
         return carry
     lax.fori_loop(0, experts, expert, 0)
 
-    noted = table.at[pl.ds(0, n - 1)]
-    pltpu.make_async_copy(noted, noted, note_recv).wait()
-    pltpu.make_async_copy(noted, noted, note_send).wait()
-    place_rows(table, me, core, n, experts, cap, place)
-    for e in range(experts):
-        pair_copy(e).wait_recv()
-
-    def chunk(j):
-        lanes = 2 * experts * cap
-        pick = one(iota((cut + rest, lanes), 0) == place[pl.ds(2 * j + core, 1), :]).astype(BF16)
-        near = rows[1, :, pl.ds(j, 1)].reshape(experts * cap, width)
-        far = theirs[:, pl.ds(j, 1)].reshape(experts * cap, width)
-        both = jnp.concatenate([near, far], axis=0)
-        return jnp.dot(pick, both, preferred_element_type=F32).astype(BF16)
-
-    def send(p, i, j):
-        return pltpu.make_async_remote_copy(
-            src_ref=(pack_a, pack_b)[p].at[i], dst_ref=(got_a, got_b)[p].at[i], send_sem=send_sem.at[p],
-            recv_sem=recv_sem.at[p], device_id={"ep": 2 * j + core}, device_id_type=MESH)
-
-    def push_first(i, carry):
-        j = step_to(chip, side, i)
-        block = chunk(j)
-        pack_a[i] = block[:cut]
-        pack_b[i] = block[cut:]
-        send(0, i, j).start()
-        return carry
-    lax.fori_loop(0, chips - 1, push_first, 0, unroll=UNROLL)
-
-    def push_rest(i, carry):
-        send(1, i, step_to(chip, side, i)).start()
-        return carry
-    lax.fori_loop(0, chips - 1, push_rest, 0)
-    block = chunk(chip)
-    got_a[chips - 1] = block[:cut]
-    got_b[chips - 1] = block[cut:]
+    wait_notes(note_send)
+    pair_copy(experts - 1).wait_recv()
+    push_block(1, experts)
 
     theirs_copy = pltpu.make_async_copy(theirs, other, theirs_sem)
     theirs_copy.start()
@@ -374,11 +398,14 @@
         def some_cols(i, carry):
             cols = pl.ds(pl.multiple_of(i * COLS, COLS), COLS)
             total[:, cols] += weigh(got, mix_ref, cols)
+            if p == 1:
+                pltpu.make_async_copy(total.at[:, cols], total_out.at[:, cols], out_sem).start()
             return carry
         lax.fori_loop(0, width // COLS, some_cols, 0, unroll=p == 1)
 
     for p, sent in enumerate((pack_a, pack_b)):
         pltpu.make_async_copy(sent, sent, send_sem.at[p]).wait()
+    pltpu.make_async_copy(total, total_out, out_sem).wait()
     for e in range(experts):
         own_copy(e).wait()
         pair_copy(e).wait_send()
@@ -413,8 +440,8 @@
     lax.fori_loop(0, chips - 1, greet, 0)
 
     def load(i, j):
-        return (pltpu.make_async_copy(own.at[:, j], src.at[i, 0], load_sem.at[i, 0]),
-                pltpu.make_async_copy(other.at[:, j], src.at[i, 1], load_sem.at[i, 1]))
+        return (pltpu.make_async_copy(own.at[:, j], src.at[i, :, 0], load_sem.at[i, 0]),
+                pltpu.make_async_copy(other.at[:, j], src.at[i, :, 1], load_sem.at[i, 1]))
 
     def load_to(i, carry):
         for copy in load(i, step_to(chip, side, i)):
@@ -473,7 +500,7 @@
         ffn = w_gate.shape[2]
         tokens, top = slot_index.shape
         most = 2 * (HEADED * (cap - HEAD) + (experts - HEADED) * cap)
-        cut = -(-ROOM // 16) * 8
+        cut = CUT
         any_spec = pl.BlockSpec(memory_space=pl.ANY)
         vmem_spec = pl.BlockSpec(memory_space=pltpu.VMEM)
         smem_spec = pl.BlockSpec(memory_space=pltpu.SMEM)
@@ -491,9 +518,16 @@
                 shape((1, 1), I32),
                 shape((tokens, width), F32),
             ),
-            in_specs=[smem_spec] + [vmem_spec] * 4 + [any_spec] * 4,
-            out_specs=(any_spec,) * 2 + (vmem_spec, smem_spec, vmem_spec),
+            in_specs=[any_spec] * 8,
+            out_specs=(any_spec,) * 2 + (vmem_spec, smem_spec, any_spec),
             scratch_shapes=[
+                pltpu.SMEM((experts, sources), I32),
+                vmem((experts, sources), I32),
+                vmem((top, tokens), I32),
+                vmem((top, tokens), I32),
+                vmem((top, tokens), F32),
+                vmem((tokens, width), F32),
+                dma((5,)), dma,
                 vmem((2, 2, chips, cap, width), BF16),
                 vmem((2, width, ffn), BF16),
                 vmem((2, width, ffn), BF16),
@@ -518,7 +552,7 @@
                 dma((3, 2)), dma((2, 2)), dma((2, ffn // COLS)), dma((experts,)), dma, dma((experts,)), dma((experts,)), dma((2,)), dma, dma, dma, dma((2,)), dma((2,)),
             ],
             compiler_params=pltpu.CompilerParams(collective_id=0, has_side_effects=True, vmem_limit_bytes=GRANT),
-        )(fill_t, fill_t, expert_t, slot_t, weight_t, dispatched.reshape(chips, 2, experts, cap, width), w_gate, w_up, w_down)
+        )(fill_t, expert_t, slot_t, weight_t, dispatched.reshape(chips, 2, experts, cap, width), w_gate, w_up, w_down)
 
         def more(room, index):
             result = pl.pallas_call(
@@ -528,7 +562,7 @@
                 in_specs=[vmem_spec] * 5 + [any_spec] * 2,
                 out_specs=vmem_spec,
                 scratch_shapes=[
-                    vmem((chips, 2, experts, cap, width), BF16),
+                    vmem((chips, experts, 2, cap, width), BF16),
                     vmem((chips - 1, room, width), BF16),
                     vmem((chips, room, width), BF16),
                     vmem((3 * tokens, chips * room), BF16),

time: 76.8 us -> 74.4 us (0.969)
  the two profiles are of different devices: /device:TPU:96 before, /device:TPU:106 now
where the time goes in v3:
time: 74.4 us; the launch traced here: 74.3 us
  Pallas kernels  71.3 us (96%)
  other arithmetic  2.09 us (3%)
    pallas_call x1, Pallas kernels, step(): pl.pallas_call(functools.partial(main_kernel, n), name='main', out_shape=...  71.3 us
    convert_element_type x1, other arithmetic, step(): total.astype(BF16)  2.09 us

profile of v3, /device:TPU:106, one launch (start us, length us, event | category | flops | bytes accessed | tf_op | source)
XLA Modules:
  0.0 74.3 jit_solution(10146798289367210504)
XLA Ops:
  0.0 71.3 %main.1 = (bf16[4,16,16,2048]{3,2,1,0:T(8,128)(2,1)}, bf16[4,16,16,2048]{3,2,1,0:T(8,128)(2,1)}, f32[32,8,128]{2,1,0:T(8,128)}, s32[1,1]{1,0:T(1,128)}, f32[128,2048]{1,0:T(8,128)}) custom-call(s32[4,32]{1,0:T(4,128)} %bitcast.25, s32[8,128]{1,0:T(8,128)} %bitcast.7, s32[8,128]{1,0:T(8,128)} %bitcast.13, f32[8,128]{1,0:T(8,128)} %bitcast.19, ...), custom_call_target="tpu_custom_call" | custom-call | tf_op jit(solution)/shard_map/main/pallas_call | solution.py:511
  72.0 0.2 conditional.4
  72.2 2.1 %convert_element_type.32 = bf16[128,2048]{1,0:T(8,128)(2,1)} convert(f32[128,2048]{1,0:T(8,128)} %get-tuple-element.138) | non-fusion elementwise | flops 262144 | bytes 1572864 | tf_op jit(solution)/shard_map/cond/branch_0_fun/convert_element_type | solution.py:578

commit v4 on v3

--- a/solution.py
+++ b/solution.py
@@ -18,7 +18,7 @@
 ROOM = 48
 MORE = (8, 16, 24, 40)
 GRANT = 64 * 1024 * 1024 - 65536
-ORDER = ((2, 2), (2, 1), (2, 3), (1, 2), (3, 2), (2, 0), (0, 2), (1, 1), (3, 3), (1, 3), (3, 1), (1, 0), (3, 0), (0, 1), (0, 3))
+ORDER = ((2, 2), (1, 2), (3, 2), (2, 1), (2, 3), (0, 2), (2, 0), (1, 1), (3, 3), (3, 1), (1, 3), (0, 1), (0, 3), (1, 0), (3, 0))
 STEP_X = sum(x << (2 * i) for i, (x, y) in enumerate(ORDER))
 STEP_Y = sum(y << (2 * i) for i, (x, y) in enumerate(ORDER))
 

time: 74.4 us -> 73.9 us (level)
  the two profiles are of different devices: /device:TPU:106 before, /device:TPU:97 now
where the time goes in v4:
time: 73.9 us; the launch traced here: 73.7 us
  Pallas kernels  70.8 us (96%)
  other arithmetic  2.09 us (3%)
    pallas_call x1, Pallas kernels, step(): pl.pallas_call(functools.partial(main_kernel, n), name='main', out_shape=...  70.8 us
    convert_element_type x1, other arithmetic, step(): total.astype(BF16)  2.09 us

profile of v4, /device:TPU:97, one launch (start us, length us, event | category | flops | bytes accessed | tf_op | source)
XLA Modules:
  0.0 73.7 jit_solution(6014937586164535381)
XLA Ops:
  0.0 70.8 %main.1 = (bf16[4,16,16,2048]{3,2,1,0:T(8,128)(2,1)}, bf16[4,16,16,2048]{3,2,1,0:T(8,128)(2,1)}, f32[32,8,128]{2,1,0:T(8,128)}, s32[1,1]{1,0:T(1,128)}, f32[128,2048]{1,0:T(8,128)}) custom-call(s32[4,32]{1,0:T(4,128)} %bitcast.25, s32[8,128]{1,0:T(8,128)} %bitcast.7, s32[8,128]{1,0:T(8,128)} %bitcast.13, f32[8,128]{1,0:T(8,128)} %bitcast.19, ...), custom_call_target="tpu_custom_call" | custom-call | tf_op jit(solution)/shard_map/main/pallas_call | solution.py:511
  71.5 0.2 conditional.4
  71.7 2.1 %convert_element_type.32 = bf16[128,2048]{1,0:T(8,128)(2,1)} convert(f32[128,2048]{1,0:T(8,128)} %get-tuple-element.138) | non-fusion elementwise | flops 262144 | bytes 1572864 | tf_op jit(solution)/shard_map/cond/branch_0_fun/convert_element_type | solution.py:578
